TPU v7x, 32 devices: a whole 2x2x4 slice. The times are simulated.
32 devices in a mesh: dp: 4 (over y, x), expert: 8 (over z, core).
Axes of the slice: x: 2, y: 2, z: 4, core: 2. Of those that a mesh axis runs over, the one named last changes fastest.
Arguments:
- tokens: bfloat16 [16384, 2048], P(('dp', 'expert')), may hold values from -6 to 6
- expert_ids: int32 [16384, 1], P(('dp', 'expert')), may hold values from 0 to 7; in each aligned block of 512 rows (0 to 511, 512 to 1023, ...) at most 128 rows name the same one
- gate_proj: bfloat16 [8, 2048, 768], P('expert'), may hold values from -0.125 to 0.125
- up_proj: bfloat16 [8, 2048, 768], P('expert'), may hold values from -0.125 to 0.125
- down_proj: bfloat16 [8, 768, 2048], P('expert'), may hold values from -0.21875 to 0.21875
Outputs:
- mixed: bfloat16 [16384, 2048], P(('dp', 'expert'))
- slot_index: int32 [16384], P(('dp', 'expert'))
Inputs may be any that keep to these rules, and one draw needn't show every extreme that they name: `expert_ids`: among the rows of one device no expert is named more than 128 times; in some devices' rows one expert is named exactly 128 times.
All inputs are finite; a program needn't handle non-finite values.
Results may differ from a plain program's by a relative error of at most 0.0046.
The roundings to bfloat16 on the way count: a program that leaves them out, or rounds other values in their place, can miss the bound.
Values may be sent and summed in bfloat16 or wider, within the bound.
A program may use at most 64 MiB of HBM per device.

v0:
```python
import jax
import jax.numpy as jnp
from jax import lax
from jax.sharding import PartitionSpec as P


def entering(part, axis, combine, identity):
    place = lax.axis_index(axis)
    gathered = lax.all_gather(part, axis)
    state = jnp.zeros_like(part) + jnp.asarray(identity, part.dtype)

    def one(hop, state):
        return combine(state, lax.dynamic_index_in_dim(gathered, hop, 0, False))

    return lax.fori_loop(0, place, one, state)


def add_counts(earlier, later):
    return earlier + later


def expert_ffn(rows, gate_proj, up_proj, down_proj):
    gate_val = jnp.dot(rows, gate_proj[0], preferred_element_type=jnp.float32)
    up_val = jnp.dot(rows, up_proj[0], preferred_element_type=jnp.float32)
    hidden = (jax.nn.silu(gate_val) * up_val).astype(jnp.bfloat16)
    return jnp.dot(hidden, down_proj[0], preferred_element_type=jnp.float32).astype(jnp.bfloat16)


def on_device(tokens, expert_ids, gate_proj, up_proj, down_proj):
    tok_rows, width = tokens.shape
    experts_all = lax.axis_size("expert")
    most = 2 * tok_rows // experts_all
    capacity = tok_rows * lax.axis_size("dp")
    choices = expert_ids[:, 0]
    onehot = (choices[:, None] == jnp.arange(experts_all, dtype=jnp.int32)[None, :]).astype(
        jnp.int32
    )
    counts = jnp.sum(onehot, axis=0)
    inner = entering(counts, "expert", add_counts, jnp.zeros_like(counts))
    totals = lax.psum(counts, "expert")
    outer = entering(totals, "dp", add_counts, jnp.zeros_like(totals))
    offset = inner + outer
    before = jnp.cumsum(onehot, axis=0) - onehot
    local_rank = jnp.sum(before * onehot, axis=1)
    global_slot = (jnp.sum(onehot * offset[None, :], axis=1) + local_rank).astype(jnp.int32)
    is_kept = global_slot < capacity
    position = choices * most + local_rank
    targets = jnp.arange(experts_all * most, dtype=jnp.int32)
    dispatch = ((targets[:, None] == position[None, :]) & is_kept[None, :]).astype(jnp.bfloat16)
    outgoing = jnp.dot(dispatch, tokens, preferred_element_type=jnp.float32).astype(jnp.bfloat16)
    outgoing = outgoing.reshape(experts_all, most, width)
    arrived = lax.all_to_all(outgoing, "expert", split_axis=0, concat_axis=0, tiled=True)
    sources, slots_here, _ = arrived.shape
    flat = arrived.reshape(sources * slots_here, width)
    returned = lax.all_to_all(
        expert_ffn(flat, gate_proj, up_proj, down_proj).reshape(sources, slots_here, width),
        "expert",
        split_axis=0,
        concat_axis=0,
        tiled=True,
    )
    flat_back = returned.reshape(experts_all * most, width)
    mixed = lax.dot_general(
        dispatch, flat_back, (((0,), (0,)), ((), ())), preferred_element_type=jnp.float32
    )
    return (mixed.astype(jnp.bfloat16), global_slot)


def solution(mesh):
    in_specs = (
        P(("dp", "expert"), None),
        P(("dp", "expert"), None),
        P("expert", None, None),
        P("expert", None, None),
        P("expert", None, None),
    )
    out_specs = (P(("dp", "expert"), None), P(("dp", "expert")))
    return jax.shard_map(
        on_device, mesh=mesh, in_specs=in_specs, out_specs=out_specs, check_vma=False
    )
```

profile of v0, /device:TPU:0, one launch (start us, length us, event | category | flops | bytes accessed | tf_op | source)
XLA Modules:
  0.0 248.1 jit_solution(10858179064858535216)
XLA Ops:
  0.6 0.0 copy-start
  0.7 1.0 convert_reduce_fusion
  1.6 1.3 dynamic-slice
  3.6 0.2 dynamic-update-slice
  3.8 10.6 %all-reduce.1 = (s32[64]{0:T(128)S(1)}, s32[1,8]{1,0:T(1,128)S(1)}) all-reduce(s32[64]{0:T(128)S(1)} %dynamic-update-slice, s32[1,8]{1,0:T(1,128)S(1)} %bitcast.49), channel_id=2, replica_groups=mesh['dp'=4,'expert'=8] {'expert'}, use_global_device_ids=true, to_apply=%add | all-reduce | flops 72 | bytes 576
  14.4 7.9 %all-gather.1 = s32[4,1,8]{2,1,0:T(1,128)S(1)} all-gather(s32[1,1,8]{2,1,0:T(1,128)S(1)} %bitcast.50), channel_id=1, replica_groups=mesh['dp'=4,'expert'=8] {'dp'}, dimensions={0}, use_global_device_ids=true | all-gather | bytes 160 | tf_op jit(solution)/shard_map/all_gather | solution.py:9
  22.4 0.1 reshape.52
  22.5 0.7 fusion.18
  23.2 1.1 reduce-window.6
  24.3 0.2 slice_reduce_fusion
  24.5 0.8 select_reduce_fusion
  25.3 0.7 multiply_add_fusion
  26.0 0.6 broadcast_compare_fusion
  26.6 3.9 %convolution_convert_fusion = bf16[1024,2048]{1,0:T(8,128)(2,1)S(1)} fusion(bf16[512,2048]{1,0:T(8,128)(2,1)} %param.9, s32[512]{0:T(512)S(1)} %multiply_add_fusion, pred[512]{0:T(512)(128)(4,1)S(1)} %get-tuple-element.70), kind=kOutput, calls=%fused_computation.2 | convolution fusion | flops 2150629376 | bytes 6294016 | tf_op jit(solution)/shard_map/dot_general | solution.py:50
  30.5 0.0 copy-start.2
  30.5 96.7 %all_to_all.10 = bf16[8,128,2048]{2,1,0:T(8,128)(2,1)S(1)} all-to-all(bf16[8,128,2048]{2,1,0:T(8,128)(2,1)S(1)} %bitcast.43), channel_id=1, replica_groups=mesh['dp'=4,'expert'=8] {'expert'}, dimensions={0} | all-to-all | bytes 8388608 | tf_op jit(solution)/shard_map/all_to_all | solution.py:52
  127.3 0.0 copy-start.1
  127.3 1.9 copy-done.1
  129.2 0.0 copy-done.2
  129.2 5.2 %fusion.1 = f32[1024,768]{1,0:T(8,128)} fusion(bf16[1024,2048]{1,0:T(8,128)(2,1)S(1)} %bitcast.40, bf16[1,2048,768]{2,1,0:T(8,128)(2,1)S(1)} %copy-done.2), kind=kOutput, calls=%fused_computation.5 | convolution fusion | flops 3221225472 | bytes 10485760 | tf_op jit(solution)/shard_map/dot_general | solution.py:24
  134.4 0.0 copy-done
  134.4 12.3 %convolution_convert_fusion.1 = bf16[1024,2048]{1,0:T(8,128)(2,1)} fusion(bf16[1,768,2048]{2,1,0:T(8,128)(2,1)S(1)} %copy-done, f32[1024,768]{1,0:T(8,128)} %fusion.1, bf16[1024,2048]{1,0:T(8,128)(2,1)} %bitcast.41, bf16[1,2048,768]{2,1,0:T(8,128)(2,1)} %param.11), kind=kOutput, calls=%fused_computation.3 | convolution fusion | flops 6449266688 | bytes 17825792 | tf_op jit(solution)/shard_map/dot_general | solution.py:26
  146.7 97.6 %all_to_all.11 = bf16[8,128,2048]{2,1,0:T(8,128)(2,1)S(1)} all-to-all(bf16[8,128,2048]{2,1,0:T(8,128)(2,1)} %bitcast.42), channel_id=1, replica_groups=mesh['dp'=4,'expert'=8] {'expert'}, dimensions={0} | all-to-all | bytes 8388608 | tf_op jit(solution)/shard_map/all_to_all | solution.py:55
  244.3 3.8 %convolution_convert_fusion.2 = bf16[512,2048]{1,0:T(8,128)(2,1)} fusion(bf16[1024,2048]{1,0:T(8,128)(2,1)S(1)} %bitcast.39, s32[512]{0:T(512)S(1)} %multiply_add_fusion, pred[512]{0:T(512)(128)(4,1)S(1)} %get-tuple-element.70), kind=kOutput, calls=%fused_computation.10 | convolution fusion | flops 2149580800 | bytes 6294016 | tf_op jit(solution)/shard_map/dot_general | solution.py:63
  (8 shorter events, 0.0 us)
Async XLA Ops:
  0.6 133.7 %copy-start = (bf16[1,768,2048]{2,1,0:T(8,128)(2,1)S(1)}, bf16[1,768,2048]{2,1,0:T(8,128)(2,1)}, u32[]{:S(2)}) copy-start(bf16[1,768,2048]{2,1,0:T(8,128)(2,1)} %param.13) | copy-start | bytes 9437188
  30.5 98.7 %copy-start.2 = (bf16[1,2048,768]{2,1,0:T(8,128)(2,1)S(1)}, bf16[1,2048,768]{2,1,0:T(8,128)(2,1)}, u32[]{:S(2)}) copy-start(bf16[1,2048,768]{2,1,0:T(8,128)(2,1)} %param.12) | copy-start | bytes 9437188
  127.3 1.9 copy-start.1
where the time goes:
time: 248 us
  blocking collectives  213 us (86%)
  matrix products  25.3 us (10%)
  other arithmetic  4.85 us (2%)
  local copies, waits for them, and re-layouts  3.79 us (2%)
    all_to_all x1, blocking collectives, on_device(): lax.all_to_all(expert_ffn(flat, gate_proj, up_proj, down_proj).reshape(so...  97.6 us
    all_to_all x1, blocking collectives, on_device(): lax.all_to_all(outgoing, 'expert', split_axis=0, concat_axis=0, tiled=True)  96.7 us
    dot_general x1, matrix products, expert_ffn(): jnp.dot(hidden, down_proj[0], preferred_element_type=jnp.float32)  12.3 us
    unnamed x1, blocking collectives  10.6 us
    all_gather x1, blocking collectives, entering(): gathered = lax.all_gather(part, axis)  7.94 us
    dot_general x1, matrix products, expert_ffn(): up_val = jnp.dot(rows, up_proj[0], preferred_element_type=jnp.float32)  5.18 us

commit v1 on v0

v1 whole, which is shorter than its diff:
```python
import functools

import jax
import jax.numpy as jnp
from jax import lax
from jax.experimental import pallas as pl
from jax.experimental.pallas import tpu as pltpu
from jax.sharding import PartitionSpec as P

MESH = pl.DeviceIdType.MESH
F32 = jnp.float32
BF16 = jnp.bfloat16
LANES = 128


def spread(step, n):
    half = (step // 2) * (2 * (step % 2) - 1)
    return jnp.where(step == 0, 0, n // 2 + half)


def kernel(
    n, dps, most, capacity,
    row_ids, col_ids, tok_ref, gate_hbm, up_hbm, down_hbm,
    out_ref, slot_ref,
    gate_ref, up_ref, down_ref, outgoing, arrived, results, returned,
    position, offset, counts, count_all, totals, total_all,
    weight_sem, go_send, go_recv, back_send, back_recv,
    count_send, count_recv, total_send, total_recv,
):
    me = lax.axis_index("expert")
    group = lax.axis_index("dp")
    tok = tok_ref.shape[0]
    width = tok_ref.shape[1]

    weights = [
        pltpu.make_async_copy(src.at[0], dst, weight_sem.at[i])
        for i, (src, dst) in enumerate(
            ((gate_hbm, gate_ref), (up_hbm, up_ref), (down_hbm, down_ref))
        )
    ]
    for copy in weights:
        copy.start()

    barrier = pltpu.get_barrier_semaphore()

    def greet(i, c):
        pl.semaphore_signal(
            barrier, inc=1, device_id={"expert": lax.rem(me + i, n)}, device_id_type=MESH
        )
        return c

    def greet_dp(i, c):
        pl.semaphore_signal(
            barrier, inc=1, device_id={"dp": lax.rem(group + i, dps)}, device_id_type=MESH
        )
        return c

    lax.fori_loop(1, n, greet, 0)
    lax.fori_loop(1, dps, greet_dp, 0)

    earlier = lax.broadcasted_iota(jnp.int32, (tok, tok), 0) < lax.broadcasted_iota(
        jnp.int32, (tok, tok), 1
    )
    later = lax.broadcasted_iota(jnp.int32, (tok, tok), 0) > lax.broadcasted_iota(
        jnp.int32, (tok, tok), 1
    )
    ids_row = row_ids[...]
    hot_row = (ids_row == lax.broadcasted_iota(jnp.int32, (n, tok), 0)).astype(F32)
    before_row = jnp.dot(
        hot_row.astype(BF16), earlier.astype(F32).astype(BF16), preferred_element_type=F32
    )
    rank_row = jnp.sum(before_row * hot_row, axis=0, keepdims=True).astype(jnp.int32)
    pos_row = ids_row * most + rank_row
    counts[...] = jnp.broadcast_to(
        jnp.sum(hot_row, axis=1, keepdims=True), (n, LANES)
    ).astype(jnp.int32)

    ids_col = col_ids[...]
    hot_col = (ids_col == lax.broadcasted_iota(jnp.int32, (tok, n), 1)).astype(F32)
    before_col = jnp.dot(
        later.astype(F32).astype(BF16), hot_col.astype(BF16), preferred_element_type=F32
    )
    rank_col = jnp.sum(before_col * hot_col, axis=1, keepdims=True).astype(jnp.int32)
    position[...] = ids_col * most + rank_col

    def go(dest, source):
        return pltpu.make_async_remote_copy(
            src_ref=outgoing.at[dest], dst_ref=arrived.at[source],
            send_sem=go_send.at[dest], recv_sem=go_recv.at[source],
            device_id={"expert": dest}, device_id_type=MESH,
        )

    def back(dest, source):
        return pltpu.make_async_remote_copy(
            src_ref=results.at[dest], dst_ref=returned.at[source],
            send_sem=back_send.at[dest], recv_sem=back_recv.at[source],
            device_id={"expert": dest}, device_id_type=MESH,
        )

    def count(dest, source):
        return pltpu.make_async_remote_copy(
            src_ref=counts, dst_ref=count_all.at[source],
            send_sem=count_send.at[dest], recv_sem=count_recv.at[source],
            device_id={"expert": dest}, device_id_type=MESH,
        )

    def total(dest, source):
        return pltpu.make_async_remote_copy(
            src_ref=totals, dst_ref=total_all.at[source],
            send_sem=total_send.at[dest], recv_sem=total_recv.at[source],
            device_id={"dp": dest}, device_id_type=MESH,
        )

    def pack(dest):
        pick = (
            lax.broadcasted_iota(jnp.int32, (most, tok), 0) + dest * most == pos_row
        ).astype(F32).astype(BF16)
        return jnp.dot(pick, tok_ref[...], preferred_element_type=F32).astype(BF16)

    pl.semaphore_wait(barrier, n + dps - 2)

    def dispatch(i, c):
        dest = lax.rem(me + spread(i, n), n)
        outgoing[dest] = pack(dest)
        go(dest, me).start()
        return c

    lax.fori_loop(1, n, dispatch, 0)

    def tell(i, c):
        count(lax.rem(me + i, n), me).start()
        return c

    lax.fori_loop(1, n, tell, 0)
    count_all[me] = counts[...]
    arrived[me] = pack(me)

    for copy in weights:
        copy.wait()

    def ffn(source):
        rows = arrived[source]
        gate = jnp.dot(rows, gate_ref[...], preferred_element_type=F32)
        up = jnp.dot(rows, up_ref[...], preferred_element_type=F32)
        hidden = (gate / (1.0 + jnp.exp(-gate)) * up).astype(BF16)
        return jnp.dot(hidden, down_ref[...], preferred_element_type=F32).astype(BF16)

    def expert_step(i, c):
        source = lax.rem(me + n - spread(i, n), n)

        @pl.when(i > 0)
        def _():
            go(me, source).wait_recv()

        results[source] = ffn(source)

        @pl.when(i > 0)
        def _():
            back(source, me).start()

        return c

    lax.fori_loop(0, n, expert_step, 0)

    def heard(i, c):
        count(me, lax.rem(me + i, n)).wait_recv()
        return c

    lax.fori_loop(1, n, heard, 0)

    def add(i, carry):
        inner, whole = carry
        here = count_all[i]
        return inner + here * (i < me).astype(jnp.int32), whole + here

    zero = jnp.zeros((n, LANES), jnp.int32)
    inner, whole = lax.fori_loop(0, n, add, (zero, zero))
    totals[...] = whole

    def tell_dp(i, c):
        total(lax.rem(group + i, dps), group).start()
        return c

    lax.fori_loop(1, dps, tell_dp, 0)
    total_all[group] = whole

    def heard_dp(i, c):
        total(group, lax.rem(group + i, dps)).wait_recv()
        return c

    lax.fori_loop(1, dps, heard_dp, 0)

    def add_dp(i, outer):
        return outer + total_all[i] * (i < group).astype(jnp.int32)

    offset[...] = inner + lax.fori_loop(0, dps, add_dp, zero)
    slot_ref[...] = (
        jnp.sum(
            hot_row * offset[:, 0:1].astype(F32), axis=0, keepdims=True
        ).astype(jnp.int32)
        + rank_row
    )

    piece = min(width, 512)

    def combine(source, block, first):
        lane = lax.broadcasted_iota(jnp.int32, (tok, most), 1)
        fits = offset[pl.ds(source, 1), 0:most] + lax.broadcasted_iota(
            jnp.int32, (1, most), 1
        ) < capacity
        pick = (lane + source * most == position[...]) & fits
        pick = pick.astype(F32).astype(BF16)
        for at in range(0, width, piece):
            part = jnp.dot(
                pick, block[source, :, at : at + piece], preferred_element_type=F32
            ).astype(BF16)
            if first:
                out_ref[:, at : at + piece] = part
            else:
                out_ref[:, at : at + piece] += part

    combine(me, results, True)

    def combine_step(i, c):
        source = lax.rem(me + n - spread(i, n), n)
        back(me, source).wait_recv()
        combine(source, returned, False)
        return c

    lax.fori_loop(1, n, combine_step, 0)

    def drain(i, c):
        other = lax.rem(me + i, n)
        go(other, me).wait_send()
        back(other, me).wait_send()
        count(other, me).wait_send()
        return c

    lax.fori_loop(1, n, drain, 0)

    def drain_dp(i, c):
        total(lax.rem(group + i, dps), group).wait_send()
        return c

    lax.fori_loop(1, dps, drain_dp, 0)


def on_device(tokens, expert_ids, gate_proj, up_proj, down_proj):
    tok, width = tokens.shape
    hidden = gate_proj.shape[2]
    n = lax.axis_size("expert")
    dps = lax.axis_size("dp")
    most = 2 * tok // n
    capacity = tok * dps
    vmem = pl.BlockSpec(memory_space=pltpu.VMEM)
    anywhere = pl.BlockSpec(memory_space=pltpu.MemorySpace.HBM)
    dma = pltpu.SemaphoreType.DMA
    block = pltpu.VMEM((n, most, width), BF16)
    mixed, slot = pl.pallas_call(
        functools.partial(kernel, n, dps, most, capacity),
        out_shape=(
            jax.ShapeDtypeStruct((tok, width), BF16),
            jax.ShapeDtypeStruct((1, tok), jnp.int32),
        ),
        in_specs=[vmem, vmem, vmem, anywhere, anywhere, anywhere],
        out_specs=(vmem, vmem),
        scratch_shapes=[
            pltpu.VMEM((width, hidden), BF16),
            pltpu.VMEM((width, hidden), BF16),
            pltpu.VMEM((hidden, width), BF16),
            block, block, block, block,
            pltpu.VMEM((tok, 1), jnp.int32),
            pltpu.VMEM((n, LANES), jnp.int32),
            pltpu.VMEM((n, LANES), jnp.int32),
            pltpu.VMEM((n, n, LANES), jnp.int32),
            pltpu.VMEM((n, LANES), jnp.int32),
            pltpu.VMEM((dps, n, LANES), jnp.int32),
            dma((3,)), dma((n,)), dma((n,)), dma((n,)), dma((n,)),
            dma((n,)), dma((n,)), dma((dps,)), dma((dps,)),
        ],
        compiler_params=pltpu.CompilerParams(
            collective_id=0, has_side_effects=True, vmem_limit_bytes=60 * 2**20
        ),
    )(
        expert_ids.reshape(1, tok), expert_ids, tokens, gate_proj, up_proj, down_proj
    )
    return mixed, slot.reshape(tok)


def solution(mesh):
    in_specs = (
        P(("dp", "expert"), None),
        P(("dp", "expert"), None),
        P("expert", None, None),
        P("expert", None, None),
        P("expert", None, None),
    )
    out_specs = (P(("dp", "expert"), None), P(("dp", "expert")))
    return jax.shard_map(
        on_device, mesh=mesh, in_specs=in_specs, out_specs=out_specs, check_vma=False
    )
```

time: 248 us -> 198 us (0.80)
  the two profiles are of different devices: /device:TPU:0 before, /device:TPU:16 now
where the time goes in v1:
time: 198 us
  Pallas kernels  192 us (97%)
  local copies, waits for them, and re-layouts  5.28 us (3%)
    pallas_call x1, Pallas kernels, on_device(): pl.pallas_call(functools.partial(kernel, n, dps, most, capacity), out_sha...  192 us
    unnamed x5, local copies, waits for them, and re-layouts  5.28 us

profile of v1, /device:TPU:16, one launch (start us, length us, event | category | flops | bytes accessed | tf_op | source)
XLA Modules:
  0.0 197.6 jit_solution(8077481508066042428)
XLA Ops:
  0.6 1.5 copy.7.col_ids
  2.2 191.7 %shard_map.68 = (bf16[512,2048]{1,0:T(8,128)(2,1)}, s32[1,512]{1,0:T(1,128)}) custom-call(s32[1,512]{1,0:T(1,128)} %bitcast.2, s32[512,1]{1,0:T(8,128)} %copy.7.col_ids, bf16[512,2048]{1,0:T(8,128)(2,1)} %tok_ref.1, bf16[1,2048,768]{2,1,0:T(8,128)(2,1)} %gate_hbm.1, bf16[1,2048,768]{2,1,0:T(8,128)(2,1)} %up_hbm.1, bf16[1,768,2048]{2,1,0:T(8,128)(2,1)} %down_hbm.1), custom_call_target="tpu_custom_call" | custom-call | tf_op jit(solution)/shard_map/pallas_call | solution.py:259
  193.8 0.0 copy-start
  193.9 3.2 %copy.10 = bf16[512,2048]{1,0:T(8,128)(2,1)} copy(bf16[512,2048]{1,0:T(8,128)(2,1)} %get-tuple-element.8) | data formatting | bytes 4194304
  197.0 0.0 copy-done
  197.0 0.6 copy.11
Async XLA Ops:
  193.8 3.2 %copy-start = (s32[1,512]{1,0:T(1,128)S(1)}, s32[1,512]{1,0:T(1,128)}, u32[]{:S(2)}) copy-start(s32[1,512]{1,0:T(1,128)} %get-tuple-element.5) | copy-start | bytes 6148

commit v2 on v1

--- a/solution.py
+++ b/solution.py
@@ -18,7 +18,7 @@
     return jnp.where(step == 0, 0, n // 2 + half)
 
 
-def kernel(
+def direct_kernel(
     n, dps, most, capacity,
     row_ids, col_ids, tok_ref, gate_hbm, up_hbm, down_hbm,
     out_ref, slot_ref,
@@ -245,7 +245,7 @@
     lax.fori_loop(1, dps, drain_dp, 0)
 
 
-def on_device(tokens, expert_ids, gate_proj, up_proj, down_proj):
+def direct(tokens, expert_ids, gate_proj, up_proj, down_proj):
     tok, width = tokens.shape
     hidden = gate_proj.shape[2]
     n = lax.axis_size("expert")
@@ -257,7 +257,7 @@
     dma = pltpu.SemaphoreType.DMA
     block = pltpu.VMEM((n, most, width), BF16)
     mixed, slot = pl.pallas_call(
-        functools.partial(kernel, n, dps, most, capacity),
+        functools.partial(direct_kernel, n, dps, most, capacity),
         out_shape=(
             jax.ShapeDtypeStruct((tok, width), BF16),
             jax.ShapeDtypeStruct((1, tok), jnp.int32),
@@ -287,6 +287,566 @@
     return mixed, slot.reshape(tok)
 
 
+def entering(part, axis, combine, identity):
+    place = lax.axis_index(axis)
+    gathered = lax.all_gather(part, axis)
+    state = jnp.zeros_like(part) + jnp.asarray(identity, part.dtype)
+
+    def one(hop, state):
+        return combine(state, lax.dynamic_index_in_dim(gathered, hop, 0, False))
+
+    return lax.fori_loop(0, place, one, state)
+
+
+def add_counts(earlier, later):
+    return earlier + later
+
+
+def expert_ffn(rows, gate_proj, up_proj, down_proj):
+    gate_val = jnp.dot(rows, gate_proj[0], preferred_element_type=jnp.float32)
+    up_val = jnp.dot(rows, up_proj[0], preferred_element_type=jnp.float32)
+    hidden = (jax.nn.silu(gate_val) * up_val).astype(jnp.bfloat16)
+    return jnp.dot(hidden, down_proj[0], preferred_element_type=jnp.float32).astype(jnp.bfloat16)
+
+
+def padded(tokens, expert_ids, gate_proj, up_proj, down_proj):
+    tok_rows, width = tokens.shape
+    experts_all = lax.axis_size("expert")
+    most = 2 * tok_rows // experts_all
+    capacity = tok_rows * lax.axis_size("dp")
+    choices = expert_ids[:, 0]
+    onehot = (choices[:, None] == jnp.arange(experts_all, dtype=jnp.int32)[None, :]).astype(
+        jnp.int32
+    )
+    counts = jnp.sum(onehot, axis=0)
+    inner = entering(counts, "expert", add_counts, jnp.zeros_like(counts))
+    totals = lax.psum(counts, "expert")
+    outer = entering(totals, "dp", add_counts, jnp.zeros_like(totals))
+    offset = inner + outer
+    before = jnp.cumsum(onehot, axis=0) - onehot
+    local_rank = jnp.sum(before * onehot, axis=1)
+    global_slot = (jnp.sum(onehot * offset[None, :], axis=1) + local_rank).astype(jnp.int32)
+    is_kept = global_slot < capacity
+    position = choices * most + local_rank
+    targets = jnp.arange(experts_all * most, dtype=jnp.int32)
+    dispatch = ((targets[:, None] == position[None, :]) & is_kept[None, :]).astype(jnp.bfloat16)
+    outgoing = jnp.dot(dispatch, tokens, preferred_element_type=jnp.float32).astype(jnp.bfloat16)
+    outgoing = outgoing.reshape(experts_all, most, width)
+    arrived = lax.all_to_all(outgoing, "expert", split_axis=0, concat_axis=0, tiled=True)
+    sources, slots_here, _ = arrived.shape
+    flat = arrived.reshape(sources * slots_here, width)
+    returned = lax.all_to_all(
+        expert_ffn(flat, gate_proj, up_proj, down_proj).reshape(sources, slots_here, width),
+        "expert",
+        split_axis=0,
+        concat_axis=0,
+        tiled=True,
+    )
+    flat_back = returned.reshape(experts_all * most, width)
+    mixed = lax.dot_general(
+        dispatch, flat_back, (((0,), (0,)), ((), ())), preferred_element_type=jnp.float32
+    )
+    return (mixed.astype(jnp.bfloat16), global_slot)
+
+
+def relay_kernel(
+    n, dps, most, base, dense, capacity,
+    row_ids, col_ids, tok_ref, gate_hbm, up_hbm, down_hbm,
+    out_ref, slot_ref, flag_ref,
+    gate_ref, up_ref, down_ref, outgoing, arrived, results, returned,
+    x_out, x_in, x_back, x_home, relay_out, relay_in,
+    position, x_position, offset, x_first, x_size, r_first, r_size,
+    counts, count_all, totals, total_all,
+    weight_sem, go_send, go_recv, back_send, back_recv,
+    over_send, over_recv, gather_send, gather_recv, x_send, x_recv,
+    count_send, count_recv, total_send, total_recv,
+):
+    me = lax.axis_index("expert")
+    group = lax.axis_index("dp")
+    tok, width = tok_ref.shape
+    hn = n // 2
+    over = most - base
+    near = lax.div(me, hn) * hn
+    far = hn - near
+    place = me - near
+    partner = far + place
+    piece = min(width, 512)
+
+    def around(i):
+        return lax.rem(place + i, hn)
+
+    weights = [
+        pltpu.make_async_copy(src.at[0], dst, weight_sem.at[i])
+        for i, (src, dst) in enumerate(
+            ((gate_hbm, gate_ref), (up_hbm, up_ref), (down_hbm, down_ref))
+        )
+    ]
+    for copy in weights:
+        copy.start()
+
+    barrier = pltpu.get_barrier_semaphore()
+
+    def greet(i, c):
+        pl.semaphore_signal(
+            barrier, inc=1, device_id={"expert": lax.rem(me + i, n)}, device_id_type=MESH
+        )
+        return c
+
+    def greet_dp(i, c):
+        pl.semaphore_signal(
+            barrier, inc=1, device_id={"dp": lax.rem(group + i, dps)}, device_id_type=MESH
+        )
+        return c
+
+    lax.fori_loop(1, n, greet, 0)
+    lax.fori_loop(1, dps, greet_dp, 0)
+
+    def iota(shape, axis):
+        return lax.broadcasted_iota(jnp.int32, shape, axis)
+
+    def ones(mask):
+        return mask.astype(F32).astype(BF16)
+
+    def dot(a, b):
+        return jnp.dot(a, b, preferred_element_type=F32)
+
+    def excess(count, half):
+        rows = iota((n, LANES), 0)
+        inside = (rows >= half) & (rows < half + hn)
+        size = jnp.where(inside, jnp.maximum(count - base, 0), 0)
+        first = dot(
+            ones(iota((n, n), 1) < iota((n, n), 0)), size.astype(F32).astype(BF16)
+        ).astype(jnp.int32)
+        return first, size
+
+    ids_row = row_ids[...]
+    hot_row = (ids_row == iota((n, tok), 0)).astype(F32)
+    before_row = dot(hot_row.astype(BF16), ones(iota((tok, tok), 0) < iota((tok, tok), 1)))
+    rank_row = jnp.sum(before_row * hot_row, axis=0, keepdims=True).astype(jnp.int32)
+    pos_row = ids_row * most + rank_row
+    mine = jnp.broadcast_to(
+        jnp.sum(hot_row, axis=1, keepdims=True), (n, LANES)
+    ).astype(jnp.int32)
+    counts[...] = mine
+    first, size = excess(mine, far)
+    x_first[...] = first
+    x_size[...] = size
+    start_row = jnp.sum(
+        hot_row * x_first[:, 0:1].astype(F32), axis=0, keepdims=True
+    ).astype(jnp.int32)
+    x_row = jnp.where(
+        (ids_row >= far) & (ids_row < far + hn) & (rank_row >= base),
+        start_row + rank_row - base, -1,
+    )
+
+    ids_col = col_ids[...]
+    hot_col = (ids_col == iota((tok, n), 1)).astype(F32)
+
+    def go(dest, source, far_off):
+        rows = pl.ds(0, base if far_off else most)
+        return pltpu.make_async_remote_copy(
+            src_ref=outgoing.at[dest, rows], dst_ref=arrived.at[source, rows],
+            send_sem=go_send.at[dest], recv_sem=go_recv.at[source],
+            device_id={"expert": dest}, device_id_type=MESH,
+        )
+
+    def back(dest, source, far_off):
+        rows = pl.ds(0, base if far_off else most)
+        return pltpu.make_async_remote_copy(
+            src_ref=results.at[dest, rows], dst_ref=returned.at[source, rows],
+            send_sem=back_send.at[dest], recv_sem=back_recv.at[source],
+            device_id={"expert": dest}, device_id_type=MESH,
+        )
+
+    def forward(dest, slot, source):
+        return pltpu.make_async_remote_copy(
+            src_ref=relay_out.at[slot], dst_ref=arrived.at[source, pl.ds(base, over)],
+            send_sem=over_send.at[slot], recv_sem=over_recv.at[source],
+            device_id={"expert": dest}, device_id_type=MESH,
+        )
+
+    def gather(dest, source, slot):
+        return pltpu.make_async_remote_copy(
+            src_ref=results.at[source, pl.ds(base, over)], dst_ref=relay_in.at[slot],
+            send_sem=gather_send.at[source], recv_sem=gather_recv.at[slot],
+            device_id={"expert": dest}, device_id_type=MESH,
+        )
+
+    def cross(which, src, dst):
+        return pltpu.make_async_remote_copy(
+            src_ref=src, dst_ref=dst,
+            send_sem=x_send.at[which], recv_sem=x_recv.at[which],
+            device_id={"expert": partner}, device_id_type=MESH,
+        )
+
+    def count(dest, source):
+        return pltpu.make_async_remote_copy(
+            src_ref=counts, dst_ref=count_all.at[source],
+            send_sem=count_send.at[dest], recv_sem=count_recv.at[source],
+            device_id={"expert": dest}, device_id_type=MESH,
+        )
+
+    def total(dest, source):
+        return pltpu.make_async_remote_copy(
+            src_ref=totals, dst_ref=total_all.at[source],
+            send_sem=total_send.at[dest], recv_sem=total_recv.at[source],
+            device_id={"dp": dest}, device_id_type=MESH,
+        )
+
+    def pack(dest, rows):
+        pick = ones(iota((rows, tok), 0) + dest * most == pos_row)
+        return dot(pick, tok_ref[...]).astype(BF16)
+
+    x_out[...] = dot(ones(iota((dense, tok), 0) == x_row), tok_ref[...]).astype(BF16)
+
+    pl.semaphore_wait(barrier, n + dps - 2)
+
+    def tell(i, c):
+        count(lax.rem(me + i, n), me).start()
+        return c
+
+    lax.fori_loop(1, n, tell, 0)
+    send_x = cross(0, x_out, x_in)
+    send_x.start()
+
+    def dispatch_near(i, c):
+        dest = near + around(i)
+        outgoing[dest] = pack(dest, most)
+        go(dest, me, False).start()
+        return c
+
+    lax.fori_loop(1, hn, dispatch_near, 0)
+
+    def dispatch_far(i, c):
+        dest = far + around(i)
+        outgoing[dest, pl.ds(0, base)] = pack(dest, base)
+        go(dest, me, True).start()
+        return c
+
+    lax.fori_loop(0, hn, dispatch_far, 0)
+    count_all[me] = mine
+    arrived[me] = pack(me, most)
+
+    before_col = dot(ones(iota((tok, tok), 0) > iota((tok, tok), 1)), hot_col.astype(BF16))
+    rank_col = jnp.sum(before_col * hot_col, axis=1, keepdims=True).astype(jnp.int32)
+    position[...] = ids_col * most + rank_col
+    lane = iota((1, n), 1)
+    size_lane = jnp.where(
+        (lane >= far) & (lane < far + hn),
+        jnp.maximum(jnp.sum(hot_col, axis=0, keepdims=True) - base, 0.0), 0.0,
+    )
+    first_lane = dot(
+        jnp.broadcast_to(size_lane, (16, n)).astype(BF16),
+        ones(iota((n, n), 0) < iota((n, n), 1)),
+    )[0:1]
+    start_col = jnp.sum(hot_col * first_lane, axis=1, keepdims=True).astype(jnp.int32)
+    x_position[...] = jnp.where(
+        (ids_col >= far) & (ids_col < far + hn) & (rank_col >= base),
+        start_col + rank_col - base, -1,
+    )
+
+    for copy in weights:
+        copy.wait()
+
+    def ffn(source):
+        rows = arrived[source]
+        gate = dot(rows, gate_ref[...])
+        up = dot(rows, up_ref[...])
+        hidden = (gate / (1.0 + jnp.exp(-gate)) * up).astype(BF16)
+        results[source] = dot(hidden, down_ref[...]).astype(BF16)
+
+    def near_step(i, c):
+        source = near + lax.rem(place + hn - i, hn)
+
+        @pl.when(i > 0)
+        def _():
+            go(me, source, False).wait_recv()
+
+        ffn(source)
+
+        @pl.when(i > 0)
+        def _():
+            back(source, me, False).start()
+
+        @pl.when(i == 0)
+        def _():
+            unpack()
+
+        return c
+
+    def unpack():
+        count(me, partner).wait_recv()
+        send_x.wait_recv()
+        first, size = excess(count_all[partner], near)
+        r_first[...] = first
+        r_size[...] = size
+
+        def one(i, c):
+            slot = around(i)
+            dest = near + slot
+            row = iota((over, dense), 0)
+            pick = (iota((over, dense), 1) == row + r_first[pl.ds(dest, 1), 0:1]) & (
+                row < r_size[pl.ds(dest, 1), 0:1]
+            )
+            block = dot(ones(pick), x_in[...]).astype(BF16)
+
+            @pl.when(i == 0)
+            def _():
+                arrived[partner, pl.ds(base, over)] = block
+
+            @pl.when(i > 0)
+            def _():
+                relay_out[slot] = block
+                forward(dest, slot, partner).start()
+
+            return c
+
+        lax.fori_loop(0, hn, one, 0)
+
+    lax.fori_loop(0, hn, near_step, 0)
+
+    def far_step(i, c):
+        slot = lax.rem(place + hn - i, hn)
+        source = far + slot
+        go(me, source, True).wait_recv()
+
+        @pl.when(i > 0)
+        def _():
+            forward(me, place, source).wait_recv()
+
+        ffn(source)
+        back(source, me, True).start()
+
+        @pl.when(i > 0)
+        def _():
+            gather(near + slot, source, place).start()
+
+        @pl.when(i == 0)
+        def _():
+            relay_in[place] = results[source, pl.ds(base, over)]
+
+        return c
+
+    lax.fori_loop(0, hn, far_step, 0)
+
+    def collect(i, c):
+        gather(me, partner, around(i)).wait_recv()
+        return c
+
+    lax.fori_loop(1, hn, collect, 0)
+    picks = []
+    for slot in range(hn):
+        column = iota((dense, over), 1)
+        pick = (
+            iota((dense, over), 0) == column + r_first[pl.ds(near + slot, 1), 0:1]
+        ) & (column < r_size[pl.ds(near + slot, 1), 0:1])
+        picks.append(ones(pick))
+    for at in range(0, width, piece):
+        acc = dot(picks[0], relay_in[0, :, at : at + piece])
+        for slot in range(1, hn):
+            acc += dot(picks[slot], relay_in[slot, :, at : at + piece])
+        x_back[:, at : at + piece] = acc.astype(BF16)
+    send_back = cross(1, x_back, x_home)
+    send_back.start()
+
+    def heard(i, c):
+        @pl.when(i != hn)
+        def _():
+            count(me, lax.rem(me + i, n)).wait_recv()
+
+        return c
+
+    lax.fori_loop(1, n, heard, 0)
+
+    def add(i, carry):
+        inner, whole, need = carry
+        here = count_all[i]
+        other = hn - lax.div(i, hn) * hn
+        rows = iota((n, LANES), 0)
+        outside = (rows >= other) & (rows < other + hn)
+        extra = jnp.sum(
+            jnp.where(outside, jnp.maximum(here - base, 0), 0), axis=0, keepdims=True
+        )
+        return (
+            inner + here * (i < me).astype(jnp.int32), whole + here, jnp.maximum(need, extra)
+        )
+
+    zero = jnp.zeros((n, LANES), jnp.int32)
+    inner, whole, need = lax.fori_loop(
+        0, n, add, (zero, zero, jnp.zeros((1, LANES), jnp.int32))
+    )
+    need = jnp.broadcast_to(need, (8, LANES))
+    totals[0] = whole
+    totals[1] = need
+
+    def tell_dp(i, c):
+        total(lax.rem(group + i, dps), group).start()
+        return c
+
+    lax.fori_loop(1, dps, tell_dp, 0)
+    total_all[group, 0] = whole
+    total_all[group, 1] = need
+
+    def heard_dp(i, c):
+        total(group, lax.rem(group + i, dps)).wait_recv()
+        return c
+
+    lax.fori_loop(1, dps, heard_dp, 0)
+
+    def add_dp(i, carry):
+        outer, most_needed = carry
+        return (
+            outer + total_all[i, 0] * (i < group).astype(jnp.int32),
+            jnp.maximum(most_needed, total_all[i, 1]),
+        )
+
+    outer, needed = lax.fori_loop(0, dps, add_dp, (zero, need))
+    offset[...] = inner + outer
+    flag_ref[...] = (needed > dense).astype(jnp.int32)
+    slot_ref[...] = (
+        jnp.sum(hot_row * offset[:, 0:1].astype(F32), axis=0, keepdims=True).astype(jnp.int32)
+        + rank_row
+    )
+
+    def combine(pick, block, first):
+        for at in range(0, width, piece):
+            part = dot(pick, block[:, at : at + piece]).astype(BF16)
+            if first:
+                out_ref[:, at : at + piece] = part
+            else:
+                out_ref[:, at : at + piece] += part
+
+    def choose(source, rows):
+        fits = offset[pl.ds(source, 1), 0:rows] + iota((1, rows), 1) < capacity
+        return ones((iota((tok, rows), 1) + source * most == position[...]) & fits)
+
+    combine(choose(me, most), results.at[me], True)
+
+    def near_back(i, c):
+        source = near + lax.rem(place + hn - i, hn)
+        back(me, source, False).wait_recv()
+        combine(choose(source, most), returned.at[source], False)
+        return c
+
+    lax.fori_loop(1, hn, near_back, 0)
+
+    def far_back(i, c):
+        source = far + lax.rem(place + hn - i, hn)
+        back(me, source, True).wait_recv()
+        combine(choose(source, base), returned.at[source, pl.ds(0, base)], False)
+        return c
+
+    lax.fori_loop(0, hn, far_back, 0)
+
+    entry = iota((1, dense), 1)
+    keep = jnp.zeros((1, dense), jnp.int32)
+    for slot in range(hn):
+        row = pl.ds(far + slot, 1)
+        rank = entry - x_first[row, 0:1]
+        inside = (rank >= 0) & (rank < x_size[row, 0:1])
+        keep += (inside & (offset[row, 0:1] + rank + base < capacity)).astype(jnp.int32)
+    send_back.wait_recv()
+    combine(
+        ones((iota((tok, dense), 1) == x_position[...]) & (keep > 0)), x_home, False
+    )
+
+    send_x.wait_send()
+    send_back.wait_send()
+
+    def drain_near(i, c):
+        slot = around(i)
+        other = near + slot
+        go(other, me, False).wait_send()
+        back(other, me, False).wait_send()
+        forward(other, slot, partner).wait_send()
+        gather(other, far + slot, place).wait_send()
+        return c
+
+    lax.fori_loop(1, hn, drain_near, 0)
+
+    def drain_far(i, c):
+        other = far + i
+        go(other, me, True).wait_send()
+        back(other, me, True).wait_send()
+        return c
+
+    lax.fori_loop(0, hn, drain_far, 0)
+
+    def drain(i, c):
+        count(lax.rem(me + i, n), me).wait_send()
+        return c
+
+    lax.fori_loop(1, n, drain, 0)
+
+    def drain_dp(i, c):
+        total(lax.rem(group + i, dps), group).wait_send()
+        return c
+
+    lax.fori_loop(1, dps, drain_dp, 0)
+
+
+def relayed(tokens, expert_ids, gate_proj, up_proj, down_proj):
+    tok, width = tokens.shape
+    hidden = gate_proj.shape[2]
+    n = lax.axis_size("expert")
+    dps = lax.axis_size("dp")
+    most = 2 * tok // n
+    base = most // 2
+    over = most - base
+    dense = 5 * most // 4
+    capacity = tok * dps
+    vmem = pl.BlockSpec(memory_space=pltpu.VMEM)
+    anywhere = pl.BlockSpec(memory_space=pltpu.MemorySpace.HBM)
+    dma = pltpu.SemaphoreType.DMA
+    block = pltpu.VMEM((n, most, width), BF16)
+    packed = pltpu.VMEM((dense, width), BF16)
+    relay = pltpu.VMEM((n // 2, over, width), BF16)
+    table = pltpu.VMEM((n, LANES), jnp.int32)
+    column = pltpu.VMEM((tok, 1), jnp.int32)
+    mixed, slot, flag = pl.pallas_call(
+        functools.partial(relay_kernel, n, dps, most, base, dense, capacity),
+        out_shape=(
+            jax.ShapeDtypeStruct((tok, width), BF16),
+            jax.ShapeDtypeStruct((1, tok), jnp.int32),
+            jax.ShapeDtypeStruct((8, LANES), jnp.int32),
+        ),
+        in_specs=[vmem, vmem, vmem, anywhere, anywhere, anywhere],
+        out_specs=(vmem, vmem, vmem),
+        scratch_shapes=[
+            pltpu.VMEM((width, hidden), BF16),
+            pltpu.VMEM((width, hidden), BF16),
+            pltpu.VMEM((hidden, width), BF16),
+            block, block, block, block,
+            packed, packed, packed, packed, relay, relay,
+            column, column, table, table, table, table, table,
+            table,
+            pltpu.VMEM((n, n, LANES), jnp.int32),
+            pltpu.VMEM((2, n, LANES), jnp.int32),
+            pltpu.VMEM((dps, 2, n, LANES), jnp.int32),
+            dma((3,)), dma((n,)), dma((n,)), dma((n,)), dma((n,)),
+            dma((n // 2,)), dma((n,)), dma((n,)), dma((n // 2,)), dma((2,)), dma((2,)),
+            dma((n,)), dma((n,)), dma((dps,)), dma((dps,)),
+        ],
+        compiler_params=pltpu.CompilerParams(
+            collective_id=0, has_side_effects=True, vmem_limit_bytes=60 * 2**20
+        ),
+    )(
+        expert_ids.reshape(1, tok), expert_ids, tokens, gate_proj, up_proj, down_proj
+    )
+    return lax.cond(
+        flag[0, 0] > 0,
+        lambda: padded(tokens, expert_ids, gate_proj, up_proj, down_proj),
+        lambda: (mixed, slot.reshape(tok)),
+    )
+
+
+def on_device(tokens, expert_ids, gate_proj, up_proj, down_proj):
+    n = lax.axis_size("expert")
+    if n == 8 and tokens.shape[0] // n % 16 == 0:
+        return relayed(tokens, expert_ids, gate_proj, up_proj, down_proj)
+    return direct(tokens, expert_ids, gate_proj, up_proj, down_proj)
+
+
 def solution(mesh):
     in_specs = (
         P(("dp", "expert"), None),

time: 198 us -> 171 us (0.86)
  the two profiles are of different devices: /device:TPU:16 before, /device:TPU:0 now
where the time goes in v2:
time: 171 us
  Pallas kernels  163 us (95%)
  local copies, waits for them, and re-layouts  6.48 us (4%)
    pallas_call x1, Pallas kernels, relayed(): pl.pallas_call(functools.partial(relay_kernel, n, dps, most, base, dense,...  163 us
    unnamed x7, local copies, waits for them, and re-layouts  5.28 us

profile of v2, /device:TPU:0, one launch (start us, length us, event | category | flops | bytes accessed | tf_op | source)
XLA Modules:
  0.0 170.9 jit_solution(11027792090489377207)
XLA Ops:
  0.6 1.5 copy.11.col_ids
  2.2 0.0 copy-start.1
  2.2 0.0 copy-start.3
  2.2 162.9 %shard_map.70 = (bf16[512,2048]{1,0:T(8,128)(2,1)}, s32[1,512]{1,0:T(1,128)S(1)}, s32[8,128]{1,0:T(8,128)}) custom-call(s32[1,512]{1,0:T(1,128)} %bitcast.47, s32[512,1]{1,0:T(8,128)} %copy.11.col_ids, bf16[512,2048]{1,0:T(8,128)(2,1)} %tok_ref.1, bf16[1,2048,768]{2,1,0:T(8,128)(2,1)} %gate_hbm.1, bf16[1,2048,768]{2,1,0:T(8,128)(2,1)} %up_hbm.1, ...), custom_call_target="tpu_custom_call" | custom-call | tf_op jit(solution)/shard_map/pallas_call | solution.py:806
  165.1 1.2 slice.9
  166.9 0.0 copy-done.1
  166.9 0.0 copy-done.3
  166.9 0.2 conditional.1
  167.2 3.2 %copy.36 = bf16[512,2048]{1,0:T(8,128)(2,1)} copy(bf16[512,2048]{1,0:T(8,128)(2,1)} %get-tuple-element.200) | data formatting | bytes 4194304
  170.3 0.6 copy.37
Async XLA Ops:
  2.2 164.8 %copy-start.1 = (bf16[1,2048,768]{2,1,0:T(8,128)(2,1)S(1)}, bf16[1,2048,768]{2,1,0:T(8,128)(2,1)}, u32[]{:S(2)}) copy-start(bf16[1,2048,768]{2,1,0:T(8,128)(2,1)} %gate_hbm.1) | copy-start | bytes 9437188
  2.2 164.8 %copy-start.3 = (s32[512,1]{0,1:T(1,128)S(1)}, s32[512,1]{0,1:T(1,128)}, u32[]{:S(2)}) copy-start(s32[512,1]{0,1:T(1,128)} %param.12) | copy-start | bytes 6148

commit v3 on v2

--- a/solution.py
+++ b/solution.py
@@ -791,9 +791,9 @@
     n = lax.axis_size("expert")
     dps = lax.axis_size("dp")
     most = 2 * tok // n
-    base = most // 2
+    base = 3 * most // 8
     over = most - base
-    dense = 5 * most // 4
+    dense = 13 * most // 8
     capacity = tok * dps
     vmem = pl.BlockSpec(memory_space=pltpu.VMEM)
     anywhere = pl.BlockSpec(memory_space=pltpu.MemorySpace.HBM)
@@ -842,7 +842,7 @@
 
 def on_device(tokens, expert_ids, gate_proj, up_proj, down_proj):
     n = lax.axis_size("expert")
-    if n == 8 and tokens.shape[0] // n % 16 == 0:
+    if n == 8 and 2 * tokens.shape[0] // n % LANES == 0:
         return relayed(tokens, expert_ids, gate_proj, up_proj, down_proj)
     return direct(tokens, expert_ids, gate_proj, up_proj, down_proj)
 

time: 171 us -> 176 us (1.029)
  Pallas kernels: 163 us -> 168 us
    pallas_call x1, Pallas kernels: 163 us -> 168 us  [relayed(): pl.pallas_call(functools.partial(relay_kernel, n, dps, most, base, dense,...]
where the time goes in v3:
time: 176 us
  Pallas kernels  168 us (95%)
  local copies, waits for them, and re-layouts  6.48 us (4%)
    pallas_call x1, Pallas kernels, relayed(): pl.pallas_call(functools.partial(relay_kernel, n, dps, most, base, dense,...  168 us
    unnamed x7, local copies, waits for them, and re-layouts  5.28 us

profile of v3, /device:TPU:0, one launch (start us, length us, event | category | flops | bytes accessed | tf_op | source)
XLA Modules:
  0.0 176.1 jit_solution(9445076184431751689)
XLA Ops:
  0.6 1.5 copy.11.col_ids
  2.2 0.0 copy-start.1
  2.2 0.0 copy-start.3
  2.2 168.1 %shard_map.70 = (bf16[512,2048]{1,0:T(8,128)(2,1)}, s32[1,512]{1,0:T(1,128)S(1)}, s32[8,128]{1,0:T(8,128)}) custom-call(s32[1,512]{1,0:T(1,128)} %bitcast.47, s32[512,1]{1,0:T(8,128)} %copy.11.col_ids, bf16[512,2048]{1,0:T(8,128)(2,1)} %tok_ref.1, bf16[1,2048,768]{2,1,0:T(8,128)(2,1)} %gate_hbm.1, bf16[1,2048,768]{2,1,0:T(8,128)(2,1)} %up_hbm.1, ...), custom_call_target="tpu_custom_call" | custom-call | tf_op jit(solution)/shard_map/pallas_call | solution.py:806
  170.3 1.2 slice.9
  172.1 0.0 copy-done.1
  172.1 0.0 copy-done.3
  172.2 0.2 conditional.1
  172.4 3.2 %copy.36 = bf16[512,2048]{1,0:T(8,128)(2,1)} copy(bf16[512,2048]{1,0:T(8,128)(2,1)} %get-tuple-element.200) | data formatting | bytes 4194304
  175.6 0.6 copy.37
Async XLA Ops:
  2.2 170.0 %copy-start.1 = (bf16[1,2048,768]{2,1,0:T(8,128)(2,1)S(1)}, bf16[1,2048,768]{2,1,0:T(8,128)(2,1)}, u32[]{:S(2)}) copy-start(bf16[1,2048,768]{2,1,0:T(8,128)(2,1)} %gate_hbm.1) | copy-start | bytes 9437188
  2.2 170.0 %copy-start.3 = (s32[512,1]{0,1:T(1,128)S(1)}, s32[512,1]{0,1:T(1,128)}, u32[]{:S(2)}) copy-start(s32[512,1]{0,1:T(1,128)} %param.12) | copy-start | bytes 6148
